TPU v7x, 32 devices: a whole 2x2x4 slice. The times are simulated.
32 devices in a mesh: pts: 8 (over y, x, core), cand: 4 (over z).
Axes of the slice: x: 2, y: 2, z: 4, core: 2. Of those that a mesh axis runs over, the one named last changes fastest.
Arguments:
- points: bfloat16 [8192, 1024], P('pts'), may hold values from -6 to 6
- weights: float32 [8192], P('pts'), may hold values from 0.5 to 5
- coverage: float32 [8192], P('pts'), may hold values from -0.5 to 1
- candidates: bfloat16 [4096, 1024], P('cand'), may hold values from -6 to 6
- picks: int32 [64], replicated, may hold values from 0 to 4095
Outputs:
- gains: float32 [4096], P('cand')
- top_gains: float32 [64], replicated
- new_coverage: float32 [8192], P('pts')
All inputs are finite; a program needn't handle non-finite values.
Results may differ from a plain program's by a relative error of at most 0.0003.
Values may be sent and summed in bfloat16 or wider, within the bound.
A program may use at most 64 MiB of HBM per device.

v0:
```python
import jax
import jax.numpy as jnp
from jax import lax
from jax.sharding import PartitionSpec as P

TOPK = 64


def joined(x, axis, combine):
    everything = lax.all_gather(x, axis)
    leading = everything[0]

    def hop(k, so_far):
        return combine(so_far, everything[k])

    return lax.fori_loop(1, lax.axis_size(axis), hop, leading)


def best_values(first, second):
    return lax.top_k(jnp.concatenate([first, second]), TOPK)[0]


def on_device(points, weights, coverage, candidates, picks):
    scale = points.shape[1] ** (-0.5)
    total = points.shape[0] * lax.axis_size("pts")
    cand_rows = candidates.shape[0]
    offset = lax.axis_index("cand") * cand_rows
    sims = jnp.dot(points, candidates.T, preferred_element_type=jnp.float32) * scale
    partial_value = (
        jnp.sum(weights[:, None] * jnp.maximum(sims - coverage[:, None], 0.0), axis=0) / total
    )
    gains = lax.psum(partial_value, "pts")
    top_gains = joined(lax.top_k(gains, TOPK)[0], "cand", best_values)
    columns = offset + jnp.arange(cand_rows, dtype=jnp.int32)
    chosen = jnp.any(picks[:, None] == columns[None, :], axis=0)
    local_best = jnp.max(jnp.where(chosen[None, :], sims, -1e30), axis=1)
    best_sim = lax.pmax(local_best, "cand")
    new_coverage = jnp.maximum(coverage, best_sim)
    return (gains, top_gains, new_coverage)


def solution(mesh):
    placed = (P("pts", None), P("pts"), P("pts"), P("cand", None), P())
    return jax.shard_map(
        on_device, mesh=mesh, in_specs=placed, out_specs=(P("cand"), P(), P("pts")), check_vma=False
    )
```

profile of v0, /device:TPU:0, one launch (start us, length us, event | category | flops | bytes accessed | tf_op | source)
XLA Modules:
  0.0 56.5 jit_solution(17969848759909569890)
XLA Ops:
  0.6 0.0 copy-start
  0.7 0.9 %compare_reduce_fusion = pred[1024]{0:T(1024)(128)(4,1)S(1)} fusion(s32[1024]{0:T(1024)S(1)} %iota_add_fusion, s32[64]{0:T(128)} %param.11), kind=kLoop, calls=%fused_computation.4 | loop fusion | flops 130048 | bytes 5376 | tf_op jit(solution)/shard_map/reduce_or | solution.py:35
  1.6 0.7 %copy-done = bf16[1024,1024]{1,0:T(8,128)(2,1)S(1)} copy-done((bf16[1024,1024]{1,0:T(8,128)(2,1)S(1)}, bf16[1024,1024]{1,0:T(8,128)(2,1)}, u32[]{:S(2)}) %copy-start) | copy-done | bytes 2097176
  2.2 0.0 copy-start.3
  2.2 0.0 copy-start.2
  2.2 4.4 %select_reduce_fusion = (f32[1024]{0:T(1024)S(1)}, f32[1024]{0:T(1024)S(1)}) fusion(pred[1024]{0:T(1024)(128)(4,1)S(1)} %compare_reduce_fusion, f32[1024]{0:T(1024)} %param.9, f32[1024]{0:T(1024)} %param.8, bf16[1024,1024]{1,0:T(8,128)(2,1)S(1)} %copy-done, bf16[1024,1024]{1,0:T(8,128)(2,1)} %param.10), kind=kOutput, calls=%fused_computation.2 | convolution fusion | flops 2154821632 | bytes 4211712 | tf_op jit(solution)/shard_map/dot_general | solution.py:28
  6.6 15.2 %psum.7 = f32[1024]{0:T(1024)S(1)} all-reduce(f32[1024]{0:T(1024)S(1)} %broadcast_multiply_fusion), channel_id=1, replica_groups=mesh['pts'=8,'cand'=4] {'pts'}, use_global_device_ids=true, to_apply=%region_1.0 | all-reduce | flops 1024 | bytes 8192 | tf_op jit(solution)/shard_map/psum | solution.py:32
  21.8 0.0 copy-start.1
  21.8 4.4 %top_k.14 = (f32[1024]{0:T(1024)S(1)}, s32[1024]{0:T(1024)}) sort(f32[1024]{0:T(1024)S(1)} %psum.7, s32[1024]{0:T(1024)S(1)} %iota.11), dimensions={0}, to_apply=%region_2.0 | sort | flops 10240 | bytes 16384 | tf_op jit(solution)/shard_map/top_k | solution.py:33
  26.2 0.0 copy-done.3
  26.2 0.6 %dynamic-slice = u32[1]{0:T(128)} dynamic-slice(u32[32]{0:T(128)S(1)} %copy-done.3, u32[]{:T(128)S(6)} %add.47), dynamic_slice_sizes={1} | dynamic-slice | bytes 12
  27.5 0.1 slice_dynamic-update-slice_fusion
  27.6 11.9 %all-reduce = f32[256]{0:T(256)S(1)} all-reduce(f32[256]{0:T(256)S(1)} %slice_dynamic-update-slice_fusion), channel_id=2, replica_groups=mesh['pts'=8,'cand'=4] {'cand'}, use_global_device_ids=true, to_apply=%add | all-reduce | flops 256 | bytes 2048
  39.5 0.1 reshape.14
  39.6 8.0 %while.15 = (s32[]{:T(128)}, f32[64]{0:T(128)S(1)}, f32[4,64]{1,0:T(4,128)S(1)}, s32[]{:T(128)}, s32[]{:T(128)}, /*index=5*/s32[]{:T(128)}) while((s32[]{:T(128)}, f32[64]{0:T(128)S(1)}, f32[4,64]{1,0:T(4,128)S(1)}, s32[]{:T(128)}, s32[]{:T(128)}, /*index=5*/s32[]{:T(128)}) %tuple.41), condition=%wide.region_5.6_spmd, body=%wide.region_3.5_spmd.sunk | while | flops 1029 | bytes 4211 | solution.py:16
  39.6 0.1 pad_maximum_fusion.2
  39.7 2.6 %top_k.22 = (f32[128]{0:T(128)S(1)}, s32[128]{0:T(128)}) sort(f32[128]{0:T(128)S(1)} %pad_maximum_fusion.2, s32[128]{0:T(128)S(1)} %iota.15), dimensions={0}, to_apply=%region_4.4 | sort | flops 896 | bytes 2048 | tf_op jit(solution)/shard_map/while/body/eval_jaxpr/top_k | solution.py:20
  42.2 0.1 pad_maximum_fusion.2
  42.3 2.6 %top_k.22 = (f32[128]{0:T(128)S(1)}, s32[128]{0:T(128)}) sort(f32[128]{0:T(128)S(1)} %pad_maximum_fusion.2, s32[128]{0:T(128)S(1)} %iota.15), dimensions={0}, to_apply=%region_4.4 | sort | flops 896 | bytes 2048 | tf_op jit(solution)/shard_map/while/body/eval_jaxpr/top_k | solution.py:20
  44.9 0.1 pad_maximum_fusion.2
  45.0 2.6 %top_k.22 = (f32[128]{0:T(128)S(1)}, s32[128]{0:T(128)}) sort(f32[128]{0:T(128)S(1)} %pad_maximum_fusion.2, s32[128]{0:T(128)S(1)} %iota.15), dimensions={0}, to_apply=%region_4.4 | sort | flops 896 | bytes 2048 | tf_op jit(solution)/shard_map/while/body/eval_jaxpr/top_k | solution.py:20
  47.5 0.0 copy-start.4
  47.5 8.3 %pmax.7 = f32[1024]{0:T(1024)S(1)} all-reduce(f32[1024]{0:T(1024)S(1)} %get-tuple-element.97), channel_id=1, replica_groups=mesh['pts'=8,'cand'=4] {'cand'}, use_global_device_ids=true, to_apply=%region_8.9 | all-reduce | flops 1024 | bytes 8192 | tf_op jit(solution)/shard_map/pmax | solution.py:37
  55.9 0.0 copy-done.2
  55.9 0.6 %max.13 = f32[1024]{0:T(1024)} maximum(f32[1024]{0:T(1024)S(1)} %copy-done.2, f32[1024]{0:T(1024)S(1)} %pmax.7) | non-fusion elementwise | flops 1024 | bytes 12288 | tf_op jit(solution)/shard_map/max | solution.py:38
  56.5 0.0 copy-done.1
  56.5 0.0 copy-done.4
  (11 shorter events, 0.0 us)
Async XLA Ops:
  0.6 1.6 %copy-start = (bf16[1024,1024]{1,0:T(8,128)(2,1)S(1)}, bf16[1024,1024]{1,0:T(8,128)(2,1)}, u32[]{:S(2)}) copy-start(bf16[1024,1024]{1,0:T(8,128)(2,1)} %param.7) | copy-start | bytes 6291460
  2.2 24.0 %copy-start.3 = (u32[32]{0:T(128)S(1)}, u32[32]{0:T(128)}, u32[]{:S(2)}) copy-start(u32[32]{0:T(128)} %constant.74) | copy-start | bytes 388
  2.2 53.6 %copy-start.2 = (f32[1024]{0:T(1024)S(1)}, f32[1024]{0:T(1024)}, u32[]{:S(2)}) copy-start(f32[1024]{0:T(1024)} %param.9) | copy-start | bytes 12292
  21.8 34.7 %copy-start.1 = (f32[1024]{0:T(1024)}, f32[1024]{0:T(1024)S(1)}, u32[]{:S(2)}) copy-start(f32[1024]{0:T(1024)S(1)} %psum.7) | copy-start | bytes 12292
  47.5 8.9 %copy-start.4 = (f32[64]{0:T(128)}, f32[64]{0:T(128)S(1)}, u32[]{:S(2)}) copy-start(f32[64]{0:T(128)S(1)} %get-tuple-element.93) | copy-start | bytes 772
where the time goes:
time: 56.7 us; the launch traced here: 56.5 us
  blocking collectives  35.4 us (62%)
  other arithmetic  13.9 us (25%)
  matrix products  4.37 us (8%)
  local copies, waits for them, and re-layouts  1.48 us (3%)
  between operations  1.34 us (2%)
    psum x1, blocking collectives, on_device(): gains = lax.psum(partial_value, 'pts')  15.2 us
    unnamed x1, blocking collectives  11.9 us
    pmax x1, blocking collectives, on_device(): best_sim = lax.pmax(local_best, 'cand')  8.34 us
    top_k x3, other arithmetic, best_values(): return lax.top_k(jnp.concatenate([first, second]), TOPK)[0]  7.7 us
    top_k x1, other arithmetic, on_device(): top_gains = joined(lax.top_k(gains, TOPK)[0], 'cand', best_values)  4.43 us
    dot_general x1, matrix products, on_device(): jnp.dot(points, candidates.T, preferred_element_type=jnp.float32) * scale  4.37 us
    unnamed x13, local copies, waits for them, and re-layouts  1.37 us

commit v1 on v0

--- a/solution.py
+++ b/solution.py
@@ -29,7 +29,9 @@
     partial_value = (
         jnp.sum(weights[:, None] * jnp.maximum(sims - coverage[:, None], 0.0), axis=0) / total
     )
-    gains = lax.psum(partial_value, "pts")
+    gains = partial_value
+    for hop_ in (1, 2, 4):
+        gains = gains + lax.ppermute(gains, "pts", [(dev, dev ^ hop_) for dev in range(8)])
     top_gains = joined(lax.top_k(gains, TOPK)[0], "cand", best_values)
     columns = offset + jnp.arange(cand_rows, dtype=jnp.int32)
     chosen = jnp.any(picks[:, None] == columns[None, :], axis=0)

time: 56.7 us -> 49.9 us (0.88)
  blocking collectives: 35.4 us -> 20.3 us
  starting transfers between devices: 0 us -> 5.43 us
  waiting for transfers between devices: 0 us -> 2.41 us
    psum x1 -> x0, blocking collectives: 15.2 us -> none  [on_device(): gains = lax.psum(partial_value, 'pts')]
    ppermute x0 -> x3, starting transfers between devices: none -> 5.43 us  [on_device(): lax.ppermute(gains, 'pts', [(dev, dev ^ hop_) for dev in range(8)])]
    unnamed x1, blocking collectives: 11.9 us -> 8.34 us
    pmax x1, blocking collectives: 8.34 us -> 11.9 us  [on_device(): best_sim = lax.pmax(local_best, 'cand')]
    ppermute x0 -> x3, waiting for transfers between devices: none -> 2.41 us  [on_device(): lax.ppermute(gains, 'pts', [(dev, dev ^ hop_) for dev in range(8)])]
  transfers between devices with their start and end apart: 0 -> 3, of which waited for: 0 -> 2; matrix products, arithmetic and copies ran while one was open for 0% -> 2% of each run, Pallas kernels for 0% -> 0%
where the time goes in v1:
time: 49.9 us; the launch traced here: 49.7 us
  blocking collectives  20.3 us (41%)
  other arithmetic  13.9 us (28%)
  starting transfers between devices  5.43 us (11%)
  matrix products  4.37 us (9%)
  waiting for transfers between devices  2.41 us (5%)
  local copies, waits for them, and re-layouts  1.98 us (4%)
  between operations  1.35 us (3%)
    pmax x1, blocking collectives, on_device(): best_sim = lax.pmax(local_best, 'cand')  11.9 us
    unnamed x1, blocking collectives  8.34 us
    top_k x3, other arithmetic, best_values(): return lax.top_k(jnp.concatenate([first, second]), TOPK)[0]  7.7 us
    ppermute x3, starting transfers between devices, on_device(): lax.ppermute(gains, 'pts', [(dev, dev ^ hop_) for dev in range(8)])  5.43 us
    top_k x1, other arithmetic, on_device(): top_gains = joined(lax.top_k(gains, TOPK)[0], 'cand', best_values)  4.43 us
    dot_general x1, matrix products, on_device(): jnp.dot(points, candidates.T, preferred_element_type=jnp.float32) * scale  4.37 us
    ppermute x3, waiting for transfers between devices, on_device(): lax.ppermute(gains, 'pts', [(dev, dev ^ hop_) for dev in range(8)])  2.41 us
    unnamed x13, local copies, waits for them, and re-layouts  1.87 us
  transfers between devices with their start and end apart: 3, of which 2 were waited for; matrix products, arithmetic and copies ran while one was open for 2% of the time, Pallas kernels for 0%

profile of v1, /device:TPU:0, one launch (start us, length us, event | category | flops | bytes accessed | tf_op | source)
XLA Modules:
  0.0 49.7 jit_solution(6435301905161215542)
XLA Ops:
  0.6 0.0 copy-start
  0.7 0.9 %compare_reduce_fusion = pred[1024]{0:T(1024)(128)(4,1)S(1)} fusion(s32[1024]{0:T(1024)S(1)} %iota_add_fusion, s32[64]{0:T(128)} %param.11), kind=kLoop, calls=%fused_computation.4 | loop fusion | flops 130048 | bytes 5376 | tf_op jit(solution)/shard_map/reduce_or | solution.py:37
  1.6 0.7 %copy-done = bf16[1024,1024]{1,0:T(8,128)(2,1)S(1)} copy-done((bf16[1024,1024]{1,0:T(8,128)(2,1)S(1)}, bf16[1024,1024]{1,0:T(8,128)(2,1)}, u32[]{:S(2)}) %copy-start) | copy-done | bytes 2097176
  2.2 0.0 copy-start.2
  2.2 0.0 copy-start.3
  2.2 4.4 %select_reduce_fusion = (f32[1024]{0:T(1024)S(1)}, f32[1024]{0:T(1024)S(1)}) fusion(pred[1024]{0:T(1024)(128)(4,1)S(1)} %compare_reduce_fusion, f32[1024]{0:T(1024)} %param.9, f32[1024]{0:T(1024)} %param.8, bf16[1024,1024]{1,0:T(8,128)(2,1)S(1)} %copy-done, bf16[1024,1024]{1,0:T(8,128)(2,1)} %param.10), kind=kOutput, calls=%fused_computation.2 | convolution fusion | flops 2154821632 | bytes 4211712 | tf_op jit(solution)/shard_map/dot_general | solution.py:28
  6.6 0.6 %collective-permute-start = (f32[1024]{0:T(1024)S(1)}, f32[1024]{0:T(1024)S(1)}, u32[]{:S(2)}, u32[]{:S(2)}) collective-permute-start(f32[1024]{0:T(1024)S(1)} %broadcast_multiply_fusion), channel_id=1, source_target_pairs={{0,4},{4,0},{8,12},{12,8},{16,20},{20,16},{24,28},{28,24},{1,5},{5... | collective-permute-start | bytes 12296 | tf_op jit(solution)/shard_map/ppermute | solution.py:34
  7.2 0.8 %collective-permute-done = f32[1024]{0:T(1024)S(1)} collective-permute-done((f32[1024]{0:T(1024)S(1)}, f32[1024]{0:T(1024)S(1)}, u32[]{:S(2)}, u32[]{:S(2)}) %collective-permute-start) | collective-permute-done | bytes 4128 | tf_op jit(solution)/shard_map/ppermute | solution.py:34
  8.0 2.8 %collective-permute-start.1 = (f32[1024]{0:T(1024)S(1)}, f32[1024]{0:T(1024)S(1)}, u32[]{:S(2)}, u32[]{:S(2)}) collective-permute-start(f32[1024]{0:T(1024)S(1)} %fusion), channel_id=1, source_target_pairs={{0,8},{4,12},{8,0},{12,4},{16,24},{20,28},{24,16},{28,20},{1,9},{5... | collective-permute-start | bytes 12296 | tf_op jit(solution)/shard_map/ppermute | solution.py:34
  10.8 1.6 %collective-permute-done.1 = f32[1024]{0:T(1024)S(1)} collective-permute-done((f32[1024]{0:T(1024)S(1)}, f32[1024]{0:T(1024)S(1)}, u32[]{:S(2)}, u32[]{:S(2)}) %collective-permute-start.1) | collective-permute-done | bytes 4128 | tf_op jit(solution)/shard_map/ppermute | solution.py:34
  12.4 2.1 %collective-permute-start.2 = (f32[1024]{0:T(1024)S(1)}, f32[1024]{0:T(1024)S(1)}, u32[]{:S(2)}, u32[]{:S(2)}) collective-permute-start(f32[1024]{0:T(1024)S(1)} %add.53), channel_id=1, source_target_pairs={{0,16},{4,20},{8,24},{12,28},{16,0},{20,4},{24,8},{28,12},{1,17},{... | collective-permute-start | bytes 12296 | tf_op jit(solution)/shard_map/ppermute | solution.py:34
  14.5 11.9 %pmax.7 = f32[1024]{0:T(1024)S(1)} all-reduce(f32[1024]{0:T(1024)S(1)} %get-tuple-element.97), channel_id=1, replica_groups=mesh['pts'=8,'cand'=4] {'cand'}, use_global_device_ids=true, to_apply=%region_7.8 | all-reduce | flops 1024 | bytes 8192 | tf_op jit(solution)/shard_map/pmax | solution.py:39
  26.4 0.0 copy-done.2
  26.4 0.6 %max.13 = f32[1024]{0:T(1024)} maximum(f32[1024]{0:T(1024)S(1)} %copy-done.2, f32[1024]{0:T(1024)S(1)} %pmax.7) | non-fusion elementwise | flops 1024 | bytes 12288 | tf_op jit(solution)/shard_map/max | solution.py:40
  27.0 0.0 copy-done.3
  27.0 0.6 %dynamic-slice = u32[1]{0:T(128)} dynamic-slice(u32[32]{0:T(128)S(1)} %copy-done.3, u32[]{:T(128)S(6)} %add.57), dynamic_slice_sizes={1} | dynamic-slice | bytes 12
  28.2 0.0 collective-permute-done.2
  28.3 0.0 copy-start.1
  28.3 4.4 %top_k.14 = (f32[1024]{0:T(1024)S(1)}, s32[1024]{0:T(1024)}) sort(f32[1024]{0:T(1024)S(1)} %add.54, s32[1024]{0:T(1024)S(1)} %iota.11), dimensions={0}, to_apply=%region_1.0 | sort | flops 10240 | bytes 16384 | tf_op jit(solution)/shard_map/top_k | solution.py:35
  32.7 0.1 slice_dynamic-update-slice_fusion
  32.8 8.3 %all-reduce = f32[256]{0:T(256)S(1)} all-reduce(f32[256]{0:T(256)S(1)} %slice_dynamic-update-slice_fusion), channel_id=2, replica_groups=mesh['pts'=8,'cand'=4] {'cand'}, use_global_device_ids=true, to_apply=%add | all-reduce | flops 256 | bytes 2048
  41.1 0.1 reshape.14
  41.2 8.0 %while.15 = (s32[]{:T(128)}, f32[64]{0:T(128)S(1)}, f32[4,64]{1,0:T(4,128)S(1)}, s32[]{:T(128)}, s32[]{:T(128)}, /*index=5*/s32[]{:T(128)}) while((s32[]{:T(128)}, f32[64]{0:T(128)S(1)}, f32[4,64]{1,0:T(4,128)S(1)}, s32[]{:T(128)}, s32[]{:T(128)}, /*index=5*/s32[]{:T(128)}) %tuple.41), condition=%wide.region_4.5_spmd, body=%wide.region_2.4_spmd.sunk | while | flops 1029 | bytes 4211 | solution.py:16
  41.2 0.1 pad_maximum_fusion.2
  41.3 2.6 %top_k.22 = (f32[128]{0:T(128)S(1)}, s32[128]{0:T(128)}) sort(f32[128]{0:T(128)S(1)} %pad_maximum_fusion.2, s32[128]{0:T(128)S(1)} %iota.15), dimensions={0}, to_apply=%region_3.3 | sort | flops 896 | bytes 2048 | tf_op jit(solution)/shard_map/while/body/eval_jaxpr/top_k | solution.py:20
  43.9 0.1 pad_maximum_fusion.2
  44.0 2.6 %top_k.22 = (f32[128]{0:T(128)S(1)}, s32[128]{0:T(128)}) sort(f32[128]{0:T(128)S(1)} %pad_maximum_fusion.2, s32[128]{0:T(128)S(1)} %iota.15), dimensions={0}, to_apply=%region_3.3 | sort | flops 896 | bytes 2048 | tf_op jit(solution)/shard_map/while/body/eval_jaxpr/top_k | solution.py:20
  46.5 0.1 pad_maximum_fusion.2
  46.6 2.6 %top_k.22 = (f32[128]{0:T(128)S(1)}, s32[128]{0:T(128)}) sort(f32[128]{0:T(128)S(1)} %pad_maximum_fusion.2, s32[128]{0:T(128)S(1)} %iota.15), dimensions={0}, to_apply=%region_3.3 | sort | flops 896 | bytes 2048 | tf_op jit(solution)/shard_map/while/body/eval_jaxpr/top_k | solution.py:20
  49.2 0.0 copy-start.4
  49.2 0.0 copy-done.1
  49.2 0.5 %copy-done.4 = f32[64]{0:T(128)} copy-done((f32[64]{0:T(128)}, f32[64]{0:T(128)S(1)}, u32[]{:S(2)}) %copy-start.4) | copy-done | bytes 280
  (14 shorter events, 0.0 us)
Async XLA Ops:
  0.6 1.6 %copy-start = (bf16[1024,1024]{1,0:T(8,128)(2,1)S(1)}, bf16[1024,1024]{1,0:T(8,128)(2,1)}, u32[]{:S(2)}) copy-start(bf16[1024,1024]{1,0:T(8,128)(2,1)} %param.7) | copy-start | bytes 6291460
  2.2 24.2 %copy-start.2 = (f32[1024]{0:T(1024)S(1)}, f32[1024]{0:T(1024)}, u32[]{:S(2)}) copy-start(f32[1024]{0:T(1024)} %param.9) | copy-start | bytes 12292
  2.2 24.8 %copy-start.3 = (u32[32]{0:T(128)S(1)}, u32[32]{0:T(128)}, u32[]{:S(2)}) copy-start(u32[32]{0:T(128)} %constant.74) | copy-start | bytes 388
  6.6 1.4 %collective-permute-start = (f32[1024]{0:T(1024)S(1)}, f32[1024]{0:T(1024)S(1)}, u32[]{:S(2)}, u32[]{:S(2)}) collective-permute-start(f32[1024]{0:T(1024)S(1)} %broadcast_multiply_fusion), channel_id=1, source_target_pairs={{0,4},{4,0},{8,12},{12,8},{16,20},{20,16},{24,28},{28,24},{1,5},{5... | collective-permute-start | bytes 12296 | tf_op jit(solution)/shard_map/ppermute | solution.py:34
  8.0 4.4 %collective-permute-start.1 = (f32[1024]{0:T(1024)S(1)}, f32[1024]{0:T(1024)S(1)}, u32[]{:S(2)}, u32[]{:S(2)}) collective-permute-start(f32[1024]{0:T(1024)S(1)} %fusion), channel_id=1, source_target_pairs={{0,8},{4,12},{8,0},{12,4},{16,24},{20,28},{24,16},{28,20},{1,9},{5... | collective-permute-start | bytes 12296 | tf_op jit(solution)/shard_map/ppermute | solution.py:34
  12.4 15.8 %collective-permute-start.2 = (f32[1024]{0:T(1024)S(1)}, f32[1024]{0:T(1024)S(1)}, u32[]{:S(2)}, u32[]{:S(2)}) collective-permute-start(f32[1024]{0:T(1024)S(1)} %add.53), channel_id=1, source_target_pairs={{0,16},{4,20},{8,24},{12,28},{16,0},{20,4},{24,8},{28,12},{1,17},{... | collective-permute-start | bytes 12296 | tf_op jit(solution)/shard_map/ppermute | solution.py:34
  28.3 20.9 %copy-start.1 = (f32[1024]{0:T(1024)}, f32[1024]{0:T(1024)S(1)}, u32[]{:S(2)}) copy-start(f32[1024]{0:T(1024)S(1)} %add.54) | copy-start | bytes 12292
  49.2 0.5 %copy-start.4 = (f32[64]{0:T(128)}, f32[64]{0:T(128)S(1)}, u32[]{:S(2)}) copy-start(f32[64]{0:T(128)S(1)} %get-tuple-element.93) | copy-start | bytes 772
